TPU v7x, 32 devices: a whole 2x2x4 slice. The times are simulated.
32 devices in a mesh: rows: 8 (over z, x), cols: 4 (over y, core).
Axes of the slice: x: 2, y: 2, z: 4, core: 2. Of those that a mesh axis runs over, the one named last changes fastest.
Arguments:
- panel: float32 [4096, 1024], P('rows'), as said below
- window_block: float32 [4096, 2048], P('rows', 'cols'), may hold values from -6 to 6
- row_live: int32 [8], replicated, may hold values 0 or 1
- window_rows: int32 [4], replicated, may hold values from 2 to 7, as said below
Outputs:
- factor: float32 [4096, 1024], P('rows')
- updated: float32 [4096, 2048], P('rows', 'cols')
Inputs may be any that keep to these rules, and one draw needn't show every extreme that they name: `window_rows`: distinct tile rows, none inside the supernode. `row_live`: the value for tile rows below 2 is ignored: those rows are always present. `panel`: the first 1024 rows hold a symmetric positive definite block.
All inputs are finite; a program needn't handle non-finite values.
Results may differ from a plain program's by a relative error of at most 0.0001.
Values sent between devices are 32-bit elements; how exact they have to be, the bound alone decides.
A program may use at most 128 MiB of HBM per device.

v0:
```python
import jax
import jax.numpy as jnp
from jax import lax
from jax.sharding import PartitionSpec as P

P_SIZE = 2
HIGHEST = lax.Precision.HIGHEST
CONTRACT = (((1,), (1,)), ((), ()))


def from_root(value, axis, source):
    kept = jnp.where(lax.axis_index(axis) == source, value, 0).astype(value.dtype)
    return lax.psum(kept, axis)


def times_trans(left, right):
    return lax.dot_general(left, right, CONTRACT, precision=HIGHEST)


def symmetric(square):
    return jnp.tril(square) + jnp.tril(square, -1).T


def factor_tile(square):
    lower_tile = jnp.linalg.cholesky(square)
    identity_tile = jnp.eye(square.shape[0], dtype=jnp.float32)
    inverse = lax.linalg.triangular_solve(lower_tile, identity_tile, left_side=True, lower=True)
    return (lower_tile, inverse)


def column(block, section, width):
    return block[:, section * width : (section + 1) * width]


def solve_row(block, super_rows, inverses, width):
    tiles_now = []
    for section in range(P_SIZE):
        update = column(block, section, width)
        for earlier in range(section):
            update = update - times_trans(tiles_now[earlier], super_rows[section][earlier])
        tiles_now.append(times_trans(update, inverses[section]))
    return jnp.concatenate(tiles_now, axis=1)


def shards(panel, window_block, row_live, window_rows):
    width = panel.shape[0]
    device_row = lax.axis_index("rows")
    device_col = lax.axis_index("cols")
    live_flag = jnp.where(device_row < P_SIZE, 1, row_live[device_row]).astype(jnp.float32)
    scaled = panel * live_flag
    target = window_rows[device_col]
    target_raw = from_root(scaled, "rows", target)
    own_tiles = []
    super_rows = []
    inverses = []
    identity_tile = jnp.eye(width, dtype=jnp.float32)
    for section in range(P_SIZE):
        square = symmetric(column(scaled, section, width))
        for earlier in range(section):
            square = square - times_trans(own_tiles[earlier], own_tiles[earlier])
        square = jnp.where(device_row == section, square, identity_tile)
        lower_tile, inverse = factor_tile(square)
        payload = jnp.concatenate(own_tiles + [inverse], axis=1)
        received = from_root(payload, "rows", section)
        earlier_tiles = [column(received, earlier, width) for earlier in range(section)]
        inverses.append(column(received, section, width))
        super_rows.append(earlier_tiles)
        update = column(scaled, section, width)
        for earlier in range(section):
            update = update - times_trans(own_tiles[earlier], earlier_tiles[earlier])
        solved = times_trans(update, inverses[section])
        solved = jnp.where(device_row == section, lower_tile, solved)
        solved = jnp.where(device_row < section, jnp.zeros_like(solved), solved)
        own_tiles.append(solved)
    own_row = jnp.concatenate(own_tiles, axis=1)
    target_row = solve_row(target_raw, super_rows, inverses, width)
    updated = window_block - times_trans(own_row, target_row)
    return (own_row, updated)


def solution(mesh):
    in_specs = (P("rows", None), P("rows", "cols"), P(), P())
    out_specs = (P("rows", None), P("rows", "cols"))
    return jax.shard_map(shards, mesh=mesh, in_specs=in_specs, out_specs=out_specs, check_vma=False)
```

profile of v0, /device:TPU:0, one launch (start us, length us, event | category | flops | bytes accessed | tf_op | source)
XLA Modules:
  0.0 616.2 jit_solution(17323084982662087415)
XLA Ops:
  12.1 3.6 broadcast_select_fusion
  23.6 11.7 %cholesky.286 = f32[128,128]{1,0:T(8,128)S(1)} custom-call(f32[128,128]{1,0:T(8,128)S(1)} %cholesky.426), custom_call_target="Cholesky" | custom-call | tf_op jit(solution)/shard_map/jit(cholesky)/cholesky | solution.py:25
  35.9 9.8 %custom-call.27 = f32[1,128,128]{1,2,0:T(8,128)S(1)} custom-call(f32[1,128,128]{2,1,0:T(8,128)S(1)} %get-tuple-element.65), custom_call_target="InvertDiagBlocksLowerTriangular" | custom-call | tf_op jit(solution)/shard_map/jit(cholesky)/cholesky | solution.py:25
  48.6 12.5 %cholesky.305 = f32[128,128]{1,0:T(8,128)} custom-call(f32[128,128]{1,0:T(8,128)S(1)} %cholesky.430), custom_call_target="Cholesky" | custom-call | tf_op jit(solution)/shard_map/jit(cholesky)/cholesky | solution.py:25
  63.0 9.8 %custom-call.28 = f32[1,128,128]{1,2,0:T(8,128)S(1)} custom-call(f32[1,128,128]{2,1,0:T(8,128)S(1)} %get-tuple-element.62), custom_call_target="InvertDiagBlocksLowerTriangular" | custom-call | tf_op jit(solution)/shard_map/jit(cholesky)/cholesky | solution.py:25
  74.4 11.7 %cholesky.326 = f32[128,128]{1,0:T(8,128)S(1)} custom-call(f32[128,128]{1,0:T(8,128)S(1)} %cholesky.435), custom_call_target="Cholesky" | custom-call | tf_op jit(solution)/shard_map/jit(cholesky)/cholesky | solution.py:25
  86.8 9.8 %custom-call.29 = f32[1,128,128]{1,2,0:T(8,128)S(1)} custom-call(f32[1,128,128]{2,1,0:T(8,128)S(1)} %get-tuple-element.59), custom_call_target="InvertDiagBlocksLowerTriangular" | custom-call | tf_op jit(solution)/shard_map/jit(cholesky)/cholesky | solution.py:25
  98.0 11.9 %cholesky.343 = f32[128,128]{1,0:T(8,128)S(1)} custom-call(f32[128,128]{1,0:T(8,128)S(1)} %convolution_subtract_fusion.14), custom_call_target="Cholesky" | custom-call | tf_op jit(solution)/shard_map/jit(cholesky)/cholesky | solution.py:25
  115.1 11.9 %while.4 = (s32[]{:T(128)}, f32[512,512]{1,0:T(8,128)}, s32[4,2]{0,1:T(2,128)S(1)}, f32[4,128,128]{2,1,0:T(8,128)S(1)}, s32[]{:T(128)}) while((s32[]{:T(128)}, f32[512,512]{1,0:T(8,128)}, s32[4,2]{0,1:T(2,128)S(1)}, f32[4,128,128]{2,1,0:T(8,128)S(1)}, s32[]{:T(128)}) %tuple.55), condition=%wide.while_cond, body=%wide.while_body.sunk | while | flops 2 | bytes 131189 | solution.py:27
  127.7 40.1 %custom-call.30 = f32[4,128,128]{1,2,0:T(8,128)S(1)} custom-call(f32[4,128,128]{2,1,0:T(8,128)} %copy-done.15), custom_call_target="InvertDiagBlocksLowerTriangular" | custom-call | tf_op jit(solution)/shard_map/triangular_solve/custom-call.3 | solution.py:27
  179.5 79.4 %all-reduce.5.cloned.1.call-done = f32[512,512]{1,0:T(8,128)} async-done(((f32[512,512]{1,0:T(8,128)}), f32[512,512]{1,0:T(8,128)}) %all-reduce.5.cloned.1.call-update) | async-done | bytes 1048592 | tf_op jit(solution)/shard_map/psum | solution.py:13
  258.9 3.6 fusion.10
  270.9 11.7 %cholesky.358 = f32[128,128]{1,0:T(8,128)S(1)} custom-call(f32[128,128]{1,0:T(8,128)S(1)} %cholesky.439), custom_call_target="Cholesky" | custom-call | tf_op jit(solution)/shard_map/jit(cholesky)/cholesky | solution.py:25
  283.2 9.8 %custom-call.31 = f32[1,128,128]{1,2,0:T(8,128)S(1)} custom-call(f32[1,128,128]{2,1,0:T(8,128)S(1)} %get-tuple-element.55), custom_call_target="InvertDiagBlocksLowerTriangular" | custom-call | tf_op jit(solution)/shard_map/jit(cholesky)/cholesky | solution.py:25
  298.1 11.9 %cholesky.377 = f32[128,128]{1,0:T(8,128)S(1)} custom-call(f32[128,128]{1,0:T(8,128)S(1)} %cholesky.443), custom_call_target="Cholesky" | custom-call | tf_op jit(solution)/shard_map/jit(cholesky)/cholesky | solution.py:25
  313.9 9.8 %custom-call.32 = f32[1,128,128]{1,2,0:T(8,128)S(1)} custom-call(f32[1,128,128]{2,1,0:T(8,128)S(1)} %get-tuple-element.52), custom_call_target="InvertDiagBlocksLowerTriangular" | custom-call | tf_op jit(solution)/shard_map/jit(cholesky)/cholesky | solution.py:25
  327.0 11.7 %cholesky.398 = f32[128,128]{1,0:T(8,128)S(1)} custom-call(f32[128,128]{1,0:T(8,128)S(1)} %cholesky.448), custom_call_target="Cholesky" | custom-call | tf_op jit(solution)/shard_map/jit(cholesky)/cholesky | solution.py:25
  340.1 10.0 %custom-call.33 = f32[1,128,128]{1,2,0:T(8,128)S(1)} custom-call(f32[1,128,128]{2,1,0:T(8,128)S(1)} %get-tuple-element.49), custom_call_target="InvertDiagBlocksLowerTriangular" | custom-call | tf_op jit(solution)/shard_map/jit(cholesky)/cholesky | solution.py:25
  352.3 11.7 %cholesky.415 = f32[128,128]{1,0:T(8,128)S(1)} custom-call(f32[128,128]{1,0:T(8,128)S(1)} %convolution_subtract_fusion.13), custom_call_target="Cholesky" | custom-call | tf_op jit(solution)/shard_map/jit(cholesky)/cholesky | solution.py:25
  370.2 11.7 %while.5 = (s32[]{:T(128)}, f32[512,512]{1,0:T(8,128)}, s32[4,2]{0,1:T(2,128)S(1)}, f32[4,128,128]{2,1,0:T(8,128)S(1)}, s32[]{:T(128)}) while((s32[]{:T(128)}, f32[512,512]{1,0:T(8,128)}, s32[4,2]{0,1:T(2,128)S(1)}, f32[4,128,128]{2,1,0:T(8,128)S(1)}, s32[]{:T(128)}) %tuple.66), condition=%wide.while_cond.clone, body=%wide.while_body.clone.sunk | while | flops 2 | bytes 131189 | solution.py:27
  382.6 40.5 %custom-call.34 = f32[4,128,128]{1,2,0:T(8,128)S(1)} custom-call(f32[4,128,128]{2,1,0:T(8,128)} %copy-done.14), custom_call_target="InvertDiagBlocksLowerTriangular" | custom-call | tf_op jit(solution)/shard_map/triangular_solve/custom-call.3 | solution.py:27
  433.4 156.2 %all-reduce.7.cloned.1.call-done = (f32[512,1024]{1,0:T(8,128)}, f32[512,1024]{1,0:T(8,128)}) async-done(((f32[512,1024]{1,0:T(8,128)}, f32[512,1024]{1,0:T(8,128)}), (f32[512,1024]{1,0:T(8,128)}, f32[512,1024]{1,0:T(8,128)})) %all-reduce.7.cloned.1.call-update) | async-done | bytes 4194320 | tf_op jit(solution)/shard_map/psum | solution.py:13
  594.7 3.5 convolution_subtract_fusion
  604.7 4.5 fusion.5
  (139 shorter events, 109.8 us)
Async XLA Ops:
  7.2 251.8 %all-reduce.5.cloned.1.call-start = ((), (), s32[]{:S(2)}) async-start(), calls=%async_computation | async-start | bytes 2097152 | tf_op jit(solution)/shard_map/psum | solution.py:13
  22.6 1.0 copy-start.9
  35.3 0.6 copy-start.13
  110.0 61.0 %copy-start = (f32[512,512]{1,0:T(8,128)}, f32[512,512]{1,0:T(8,128)S(1)}, u32[]{:S(2)}) copy-start(f32[512,512]{1,0:T(8,128)S(1)} %get-tuple-element.57) | copy-start | bytes 3145732
  127.0 0.7 copy-start.15
  167.9 3.5 copy-start.1
  176.1 2.0 copy-start.7
  177.7 411.9 %all-reduce.7.cloned.1.call-start = ((), (), s32[]{:S(2)}) async-start(), calls=%async_computation.1 | async-start | bytes 8388608 | tf_op jit(solution)/shard_map/psum | solution.py:13
  258.9 3.6 copy-start.6
  269.9 1.0 copy-start.8
  282.6 0.6 copy-start.12
  381.9 0.7 copy-start.14
  423.1 3.5 copy-start.2
  589.5 3.2 copy-start.5
  589.5 3.3 copy-start.10
  592.8 1.9 copy-start.4
  603.5 1.2 copy-start.11
  604.7 4.5 copy-start.3
Sparse Core Ops, SparseCore 0:
  177.8 81.0 all-reduce.4
  433.5 156.0 all-reduce.6
where the time goes:
time: 626 us; the launch traced here: 616 us
  other arithmetic  258 us (41%)
  waiting for transfers between devices  236 us (38%)
  matrix products  56.8 us (9%)
  local copies, waits for them, and re-layouts  44.3 us (7%)
  between operations  21 us (3%)
    psum x2, waiting for transfers between devices, from_root(): return lax.psum(kept, axis)  236 us
    another operation x29, other arithmetic, factor_tile(): lower_tile = jnp.linalg.cholesky(square)  162 us
    another operation x5, other arithmetic, factor_tile(): lax.linalg.triangular_solve(lower_tile, identity_tile, left_side=True, lo...  84.1 us
    dot_general x8, matrix products, times_trans(): return lax.dot_general(left, right, CONTRACT, precision=HIGHEST)  24.9 us
    another operation x27, local copies, waits for them, and re-layouts, factor_tile(): lax.linalg.triangular_solve(lower_tile, identity_tile, left_side=True, lo...  23.5 us
    another operation x14, matrix products, factor_tile(): lax.linalg.triangular_solve(lower_tile, identity_tile, left_side=True, lo...  17.2 us
    another operation x12, matrix products, factor_tile(): lower_tile = jnp.linalg.cholesky(square)  14.7 us
  transfers between devices with their start and end apart: 2, of which 2 were waited for; matrix products, arithmetic and copies ran while one was open for 0% of the time, Pallas kernels for 0%

commit v1 on v0

--- a/solution.py
+++ b/solution.py
@@ -10,7 +10,7 @@
 
 def from_root(value, axis, source):
     kept = jnp.where(lax.axis_index(axis) == source, value, 0).astype(value.dtype)
-    return lax.psum(kept, axis)
+    return jnp.sum(lax.all_gather(kept, axis), axis=0)
 
 
 def times_trans(left, right):

time: 626 us -> 810 us (1.29)
  waiting for transfers between devices: 236 us -> 371 us
  other arithmetic: 258 us -> 281 us
  local copies, waits for them, and re-layouts: 44.3 us -> 66.6 us
    all_gather x0 -> x3, waiting for transfers between devices: none -> 370 us  [from_root(): return jnp.sum(lax.all_gather(kept, axis), axis=0)]
    psum x2 -> x0, waiting for transfers between devices: 236 us -> none  [from_root(): return lax.psum(kept, axis)]
    unnamed x33 -> x38, local copies, waits for them, and re-layouts: 7.05 us -> 29.9 us
    reduce_sum x0 -> x3, other arithmetic: none -> 21.6 us  [from_root(): return jnp.sum(lax.all_gather(kept, axis), axis=0)]
  transfers between devices with their start and end apart: 2 -> 3, of which waited for: 2 -> 3; matrix products, arithmetic and copies ran while one was open for 0% -> 26% of each run, Pallas kernels for 0% -> 0%
where the time goes in v1:
time: 810 us; the launch traced here: 799 us
  waiting for transfers between devices  371 us (46%)
  other arithmetic  281 us (35%)
  local copies, waits for them, and re-layouts  66.6 us (8%)
  matrix products  59.8 us (7%)
  between operations  21.1 us (3%)
    all_gather x3, waiting for transfers between devices, from_root(): return jnp.sum(lax.all_gather(kept, axis), axis=0)  370 us
    another operation x29, other arithmetic, factor_tile(): lower_tile = jnp.linalg.cholesky(square)  162 us
    another operation x5, other arithmetic, factor_tile(): lax.linalg.triangular_solve(lower_tile, identity_tile, left_side=True, lo...  83.7 us
    unnamed x38, local copies, waits for them, and re-layouts  29.9 us
    dot_general x8, matrix products, times_trans(): return lax.dot_general(left, right, CONTRACT, precision=HIGHEST)  28.6 us
    another operation x27, local copies, waits for them, and re-layouts, factor_tile(): lax.linalg.triangular_solve(lower_tile, identity_tile, left_side=True, lo...  23.4 us
    reduce_sum x3, other arithmetic, from_root(): return jnp.sum(lax.all_gather(kept, axis), axis=0)  21.6 us
    another operation x14, matrix products, factor_tile(): lax.linalg.triangular_solve(lower_tile, identity_tile, left_side=True, lo...  17.3 us
  transfers between devices with their start and end apart: 3, of which 3 were waited for; matrix products, arithmetic and copies ran while one was open for 26% of the time, Pallas kernels for 0%

profile of v1, /device:TPU:0, one launch (start us, length us, event | category | flops | bytes accessed | tf_op | source)
XLA Modules:
  0.0 799.3 jit_solution(14086614450274021821)
XLA Ops:
  26.2 11.7 %cholesky.286 = f32[128,128]{1,0:T(8,128)S(1)} custom-call(f32[128,128]{1,0:T(8,128)S(1)} %cholesky.426), custom_call_target="Cholesky" | custom-call | tf_op jit(solution)/shard_map/jit(cholesky)/cholesky | solution.py:25
  38.6 9.8 %custom-call.27 = f32[1,128,128]{1,2,0:T(8,128)S(1)} custom-call(f32[1,128,128]{2,1,0:T(8,128)S(1)} %get-tuple-element.63), custom_call_target="InvertDiagBlocksLowerTriangular" | custom-call | tf_op jit(solution)/shard_map/jit(cholesky)/cholesky | solution.py:25
  51.3 12.3 %cholesky.305 = f32[128,128]{1,0:T(8,128)} custom-call(f32[128,128]{1,0:T(8,128)S(1)} %cholesky.430), custom_call_target="Cholesky" | custom-call | tf_op jit(solution)/shard_map/jit(cholesky)/cholesky | solution.py:25
  65.7 9.8 %custom-call.28 = f32[1,128,128]{1,2,0:T(8,128)S(1)} custom-call(f32[1,128,128]{2,1,0:T(8,128)S(1)} %get-tuple-element.60), custom_call_target="InvertDiagBlocksLowerTriangular" | custom-call | tf_op jit(solution)/shard_map/jit(cholesky)/cholesky | solution.py:25
  77.1 11.7 %cholesky.326 = f32[128,128]{1,0:T(8,128)S(1)} custom-call(f32[128,128]{1,0:T(8,128)S(1)} %cholesky.435), custom_call_target="Cholesky" | custom-call | tf_op jit(solution)/shard_map/jit(cholesky)/cholesky | solution.py:25
  89.5 9.8 %custom-call.29 = f32[1,128,128]{1,2,0:T(8,128)S(1)} custom-call(f32[1,128,128]{2,1,0:T(8,128)S(1)} %get-tuple-element.57), custom_call_target="InvertDiagBlocksLowerTriangular" | custom-call | tf_op jit(solution)/shard_map/jit(cholesky)/cholesky | solution.py:25
  100.8 12.1 %cholesky.343 = f32[128,128]{1,0:T(8,128)S(1)} custom-call(f32[128,128]{1,0:T(8,128)S(1)} %convolution_subtract_fusion.14), custom_call_target="Cholesky" | custom-call | tf_op jit(solution)/shard_map/jit(cholesky)/cholesky | solution.py:25
  118.2 11.9 %while.4 = (s32[]{:T(128)}, f32[512,512]{1,0:T(8,128)}, s32[4,2]{0,1:T(2,128)S(1)}, f32[4,128,128]{2,1,0:T(8,128)S(1)}, s32[]{:T(128)}) while((s32[]{:T(128)}, f32[512,512]{1,0:T(8,128)}, s32[4,2]{0,1:T(2,128)S(1)}, f32[4,128,128]{2,1,0:T(8,128)S(1)}, s32[]{:T(128)}) %tuple.55), condition=%wide.while_cond, body=%wide.while_body.sunk | while | flops 2 | bytes 131189 | solution.py:27
  130.9 40.1 %custom-call.30 = f32[4,128,128]{1,2,0:T(8,128)S(1)} custom-call(f32[4,128,128]{2,1,0:T(8,128)} %copy-done.16), custom_call_target="InvertDiagBlocksLowerTriangular" | custom-call | tf_op jit(solution)/shard_map/triangular_solve/custom-call.3 | solution.py:27
  183.4 124.8 %all-gather.8.cloned.1.call-done = f32[4096,512]{1,0:T(8,128)} async-done(((f32[512,512]{1,0:T(8,128)}), f32[4096,512]{1,0:T(8,128)}) %all-gather.8.cloned.1.call-update) | async-done | bytes 8388624 | tf_op jit(solution)/shard_map/all_gather | solution.py:13
  327.1 11.7 %cholesky.358 = f32[128,128]{1,0:T(8,128)S(1)} custom-call(f32[128,128]{1,0:T(8,128)S(1)} %cholesky.439), custom_call_target="Cholesky" | custom-call | tf_op jit(solution)/shard_map/jit(cholesky)/cholesky | solution.py:25
  339.4 10.0 %custom-call.31 = f32[1,128,128]{1,2,0:T(8,128)S(1)} custom-call(f32[1,128,128]{2,1,0:T(8,128)S(1)} %get-tuple-element.53), custom_call_target="InvertDiagBlocksLowerTriangular" | custom-call | tf_op jit(solution)/shard_map/jit(cholesky)/cholesky | solution.py:25
  353.0 11.7 %cholesky.377 = f32[128,128]{1,0:T(8,128)S(1)} custom-call(f32[128,128]{1,0:T(8,128)S(1)} %cholesky.443), custom_call_target="Cholesky" | custom-call | tf_op jit(solution)/shard_map/jit(cholesky)/cholesky | solution.py:25
  368.0 9.8 %custom-call.32 = f32[1,128,128]{1,2,0:T(8,128)S(1)} custom-call(f32[1,128,128]{2,1,0:T(8,128)S(1)} %get-tuple-element.50), custom_call_target="InvertDiagBlocksLowerTriangular" | custom-call | tf_op jit(solution)/shard_map/jit(cholesky)/cholesky | solution.py:25
  381.2 12.1 %cholesky.398 = f32[128,128]{1,0:T(8,128)S(1)} custom-call(f32[128,128]{1,0:T(8,128)S(1)} %cholesky.448), custom_call_target="Cholesky" | custom-call | tf_op jit(solution)/shard_map/jit(cholesky)/cholesky | solution.py:25
  393.9 9.8 %custom-call.33 = f32[1,128,128]{1,2,0:T(8,128)S(1)} custom-call(f32[1,128,128]{2,1,0:T(8,128)S(1)} %get-tuple-element.47), custom_call_target="InvertDiagBlocksLowerTriangular" | custom-call | tf_op jit(solution)/shard_map/jit(cholesky)/cholesky | solution.py:25
  406.0 11.7 %cholesky.415 = f32[128,128]{1,0:T(8,128)S(1)} custom-call(f32[128,128]{1,0:T(8,128)S(1)} %convolution_subtract_fusion.13), custom_call_target="Cholesky" | custom-call | tf_op jit(solution)/shard_map/jit(cholesky)/cholesky | solution.py:25
  425.9 11.8 %while.5 = (s32[]{:T(128)}, f32[512,512]{1,0:T(8,128)}, s32[4,2]{0,1:T(2,128)S(1)}, f32[4,128,128]{2,1,0:T(8,128)S(1)}, s32[]{:T(128)}) while((s32[]{:T(128)}, f32[512,512]{1,0:T(8,128)}, s32[4,2]{0,1:T(2,128)S(1)}, f32[4,128,128]{2,1,0:T(8,128)S(1)}, s32[]{:T(128)}) %tuple.67), condition=%wide.while_cond.clone, body=%wide.while_body.clone.sunk | while | flops 2 | bytes 131189 | solution.py:27
  438.4 40.1 %custom-call.34 = f32[4,128,128]{1,2,0:T(8,128)S(1)} custom-call(f32[4,128,128]{2,1,0:T(8,128)} %copy-done.17), custom_call_target="InvertDiagBlocksLowerTriangular" | custom-call | tf_op jit(solution)/shard_map/triangular_solve/custom-call.3 | solution.py:27
  488.8 47.6 %all-gather.10.cloned.1.call-done = f32[4096,1024]{0,1:T(8,128)} async-done(((f32[512,1024]{0,1:T(8,128)}), f32[4096,1024]{0,1:T(8,128)}) %all-gather.10.cloned.1.call-update) | async-done | bytes 16777232 | tf_op jit(solution)/shard_map/all_gather | solution.py:13
  536.4 19.1 %copy.62 = f32[128,8,8,512]{3,2,1,0:T(8,128)S(1)} copy(f32[128,8,8,512]{3,1,2,0:T(8,128)} %bitcast.121) | data formatting | bytes 33554432
  555.6 6.9 bitcast_reduce_fusion
  566.7 197.4 %all-gather.6.cloned.1.call-done = f32[8,512,1024]{2,1,0:T(8,128)} async-done(((f32[1,512,1024]{2,1,0:T(8,128)}), f32[8,512,1024]{2,1,0:T(8,128)}) %all-gather.6.cloned.1.call-update) | async-done | bytes 16777232 | tf_op jit(solution)/shard_map/all_gather | solution.py:13
  764.1 9.3 %reduce_sum.28 = f32[512,1024]{1,0:T(8,128)} reduce(f32[8,512,1024]{2,1,0:T(8,128)} %all-gather.6.cloned.1.call-done, f32[]{:T(128)} %constant.127.clone.1), dimensions={0}, to_apply=%region_9.12 | reduce | flops 3670016 | bytes 18874372 | tf_op jit(solution)/shard_map/reduce_sum | solution.py:13
  (152 shorter events, 138.4 us)
Async XLA Ops:
  7.2 301.0 %all-gather.8.cloned.1.call-start = ((), (), s32[]{:S(2)}) async-start(), calls=%async_computation.1 | async-start | bytes 9437184 | tf_op jit(solution)/shard_map/all_gather | solution.py:13
  25.2 1.0 copy-start.10
  37.9 0.6 copy-start.14
  112.9 61.2 %copy-start.1 = (f32[512,512]{1,0:T(8,128)}, f32[512,512]{1,0:T(8,128)S(1)}, u32[]{:S(2)}) copy-start(f32[512,512]{1,0:T(8,128)S(1)} %get-tuple-element.55) | copy-start | bytes 3145732
  130.2 0.7 copy-start.16
  171.0 3.5 copy-start.3
  180.8 1.2 copy-start.8
  180.8 355.6 %all-gather.10.cloned.1.call-start = ((), (), s32[]{:S(2)}) async-start(), calls=%async_computation.2 | async-start | bytes 18874368 | tf_op jit(solution)/shard_map/all_gather | solution.py:13
  181.6 582.5 %all-gather.6.cloned.1.call-start = ((), (), s32[]{:S(2)}) async-start(), calls=%async_computation | async-start | bytes 18874368 | tf_op jit(solution)/shard_map/all_gather | solution.py:13
  313.6 5.1 copy-start.9
  326.1 1.0 copy-start.11
  338.8 0.6 copy-start.15
  352.3 0.7 copy-start.13
  437.7 0.7 copy-start.17
  478.5 3.5 copy-start.4
  555.6 8.3 %copy-start.2 = (f32[512,512]{1,0:T(8,128)S(1)}, f32[512,512]{1,0:T(8,128)}, u32[]{:S(2)}) copy-start(f32[512,512]{1,0:T(8,128)} %reduce_sum.27) | copy-start | bytes 3145732
  562.5 1.4 copy-start.6
  773.4 3.2 copy-start
  773.4 3.3 copy-start.5
  786.6 1.2 copy-start.12
  787.8 4.5 copy-start.7
Sparse Core Ops, SparseCore 0:
  181.0 127.1 all-gather.7
  310.9 225.4 all-gather.9
  538.6 225.4 all-gather.5
